TPU v7x, 32 devices: a whole 2x2x4 slice. The times are simulated.
32 devices in a mesh: section: 4 (over y, x), dp: 8 (over z, core).
Axes of the slice: x: 2, y: 2, z: 4, core: 2. Of those that a mesh axis runs over, the one named last changes fastest.
Arguments:
- clip_pool: bfloat16 [256, 256, 512], P('dp'), may hold values from -8 to 8
- clip_index: int32 [8, 32], P(None, 'dp'), may hold values from 0 to 31, as said below
- batch_order: int32 [8], replicated, may hold values from 0 to 7, each once
- tap_weights: bfloat16 [4, 3, 512, 512], P('section'), may hold values from -0.15625 to 0.15625
- out_weights: bfloat16 [4, 512, 512], P('section'), may hold values from -0.25 to 0.25
- norm_gains: bfloat16 [4, 512], P('section'), may hold values from 0.099609375 to 1.8984375
- quant_weight: bfloat16 [512, 18], replicated, may hold values from -0.25 to 0.25
- quant_bias: float32 [18], replicated, may hold values from -3 to 3
- post_weight: bfloat16 [18, 512], replicated, may hold values from -1.5 to 1.5
Outputs:
- row_error: float32 [8, 32, 256], P('section', 'dp')
- entropy_loss: float32 [8], replicated
Inputs may be any that keep to these rules, and one draw needn't show every extreme that they name: `clip_index`: entries index the clips of the replica that holds the column; over all 8 micro-batches, the 4 columns of one replica name each of its 32 clips exactly once. `batch_order`: each micro-batch number 0 to 7 once.
All inputs are finite; a program needn't handle non-finite values.
Results may differ from a plain program's by a relative error of at most 0.0015.
Values may be sent and summed in bfloat16 or wider, within the bound.
A program may use at most 128 MiB of HBM per device.

v0:
```python
import jax
import jax.numpy as jnp
from jax import lax
from jax.sharding import PartitionSpec as P

SPATIAL = 64


norm_eps = 1e-06
quant_section = 1


def run_block(current, tap_set, out_weight, gain_row):
    clip_count, row_count, channels = current.shape
    widened = current.astype(jnp.float32)
    scale = lax.rsqrt(jnp.mean(widened * widened, axis=-1, keepdims=True) + norm_eps)
    normed = (widened * scale * gain_row.astype(jnp.float32)).astype(jnp.bfloat16)
    flat = normed.reshape(-1, channels)
    mixed = jnp.zeros((clip_count, row_count, channels), jnp.float32)
    for k in range(tap_set.shape[0]):
        product = jnp.dot(flat, tap_set[k], preferred_element_type=jnp.float32).reshape(
            clip_count, row_count, channels
        )
        moved = jnp.pad(product, ((0, 0), (k * SPATIAL, 0), (0, 0)))[:, :row_count]
        mixed = mixed + moved
    activated = jax.nn.silu(mixed).astype(jnp.bfloat16)
    update = jnp.dot(
        activated.reshape(-1, channels), out_weight, preferred_element_type=jnp.float32
    )
    return (widened + update.reshape(clip_count, row_count, channels)).astype(jnp.bfloat16)


def quantize(current, quant_weight, quant_bias, post_weight):
    channels = current.shape[-1]
    logits = (
        jnp.dot(current.reshape(-1, channels), quant_weight, preferred_element_type=jnp.float32)
        + quant_bias
    )
    bit_prob = jax.nn.sigmoid(4.0 * logits)
    codes = (2.0 * bit_prob - 1.0).astype(jnp.bfloat16)
    quantized = jnp.dot(codes, post_weight, preferred_element_type=jnp.float32).astype(jnp.bfloat16)
    bit_sums = jnp.sum(bit_prob, axis=0)
    entropy_sum = -jnp.sum(
        bit_prob * jax.nn.log_sigmoid(4.0 * logits)
        + (1.0 - bit_prob) * jax.nn.log_sigmoid(-4.0 * logits)
    )
    return (quantized.reshape(current.shape), bit_sums, entropy_sum)


def squared_error(decoded, source):
    differ = decoded.astype(jnp.float32) - source.astype(jnp.float32)
    return jnp.mean(differ * differ, axis=-1)


def final_entropy(bit_buffer, entropy_buffer, batch_order, rows_total):
    marginal = bit_buffer / rows_total
    sample_entropy = entropy_buffer / rows_total
    averaged = jnp.zeros_like(marginal)
    running = marginal[batch_order[0]]
    for t in range(batch_order.shape[0]):
        if t > 0:
            running = 0.5 * running + 0.5 * marginal[batch_order[t]]
        averaged = averaged.at[batch_order[t]].set(running)
    smoothed = 0.05 + 0.9 * averaged
    code_entropy = -jnp.sum(
        smoothed * jnp.log(smoothed) + (1.0 - smoothed) * jnp.log(1.0 - smoothed), axis=-1
    )
    return sample_entropy - code_entropy


def on_device(
    clip_pool,
    clip_index,
    batch_order,
    tap_weights,
    out_weights,
    norm_gains,
    quant_weight,
    quant_bias,
    post_weight,
):
    section_id = lax.axis_index("section")
    sections = lax.axis_size("section")
    batches = batch_order.shape[0]
    clip_count = clip_index.shape[1]
    row_count = clip_pool.shape[1]
    rows_total = float(clip_count * lax.axis_size("dp") * row_count)
    bit_buffer = jnp.zeros((batches, quant_weight.shape[1]), jnp.float32)
    entropy_buffer = jnp.zeros((batches,), jnp.float32)
    all_taps, all_out, all_gains = (
        lax.all_gather(tap_weights, "section", axis=0, tiled=True),
        lax.all_gather(out_weights, "section", axis=0, tiled=True),
        lax.all_gather(norm_gains, "section", axis=0, tiled=True),
    )
    per_section = batches // sections
    error_list = []
    for i in range(per_section):
        batch_slot = section_id * per_section + i
        source = jnp.take(clip_pool, clip_index[batch_slot], axis=0)
        current = source
        for s in range(sections):
            current = run_block(current, all_taps[s], all_out[s], all_gains[s])
            if s == quant_section:
                current, bit_sums, entropy_sum = quantize(
                    current, quant_weight, quant_bias, post_weight
                )
                bit_buffer = bit_buffer.at[batch_slot].add(bit_sums)
                entropy_buffer = entropy_buffer.at[batch_slot].add(entropy_sum)
        error_list.append(squared_error(current, source))
    bit_buffer, entropy_buffer = lax.psum((bit_buffer, entropy_buffer), ("section", "dp"))
    error_out = jnp.stack(error_list)
    losses = final_entropy(bit_buffer, entropy_buffer, batch_order, rows_total)
    return (error_out, losses)


def solution(mesh):
    placed = (
        P("dp", None, None),
        P(None, "dp"),
        P(),
        P("section", None, None, None),
        P("section", None, None),
        P("section", None),
        P(),
        P(),
        P(),
    )
    return jax.shard_map(
        on_device,
        mesh=mesh,
        in_specs=placed,
        out_specs=(P("section", "dp", None), P()),
        check_vma=False,
    )
```

profile of v0, /device:TPU:0, one launch (start us, length us, event | category | flops | bytes accessed | tf_op | source)
XLA Modules:
  0.0 263.3 jit_solution(17527668626507960612)
XLA Ops:
  20.1 4.9 %gather_fusion = bf16[4,256,512]{2,1,0:T(8,128)(2,1)S(1)} fusion(bf16[32,256,512]{2,1,0:T(8,128)(2,1)} %param.35, s32[1024]{0:T(1024)S(1)} %pad_clamp_fusion.1), kind=kCustom, calls=%fused_computation.clone | custom fusion | bytes 2097168 | tf_op jit(solution)/shard_map/jit(_take)/gather | solution.py:99
  25.0 4.4 %gather_fusion.1 = bf16[4,256,512]{2,1,0:T(8,128)(2,1)S(1)} fusion(bf16[32,256,512]{2,1,0:T(8,128)(2,1)} %param.35, s32[1024]{0:T(1024)S(1)} %pad_clamp_fusion), kind=kCustom, calls=%fused_computation.1.clone | custom fusion | bytes 2097168 | tf_op jit(solution)/shard_map/jit(_take)/gather | solution.py:99
  34.6 9.3 %all-gather = bf16[4,1,512]{2,1,0:T(2,128)(2,1)S(1)} all-gather(bf16[1,1,512]{2,1,0:T(2,128)(2,1)S(1)} %bitcast.176), channel_id=1, replica_groups=mesh['section'=4,'dp'=8] {'section'}, dimensions={0}, use_global_device_ids=true | all-gather | bytes 5120 | tf_op jit(solution)/shard_map/all_gather | solution.py:93
  46.5 36.1 %all-gather.4.cloned.1.call-done = bf16[4,3,512,512]{3,2,1,0:T(8,128)(2,1)} async-done(((bf16[1,3,512,512]{3,2,1,0:T(8,128)(2,1)}), bf16[4,3,512,512]{3,2,1,0:T(8,128)(2,1)}) %all-gather.4.cloned.1.call-update) | async-done | bytes 6291472 | tf_op jit(solution)/shard_map/all_gather | solution.py:91
  82.7 3.1 %fusion.60 = f32[4,256,512]{2,1,0:T(8,128)} fusion(f32[4,256]{1,0:T(4,128)S(1)} %add_rsqrt_fusion.3, f32[512]{0:T(512)S(1)} %bitcast.189, bf16[4,3,512,512]{3,2,1,0:T(8,128)(2,1)} %all-gather.4.cloned.1.call-done, bf16[4,256,512]{2,1,0:T(8,128)(2,1)S(1)} %gather_fusion.1, pred[4]{0:T(512)(128)(4,1)S(1)} %get-tuple-element.203), kind=kOutput, calls=%fused_computation.107 | convolution fusion | flops 539492352 | bytes 3676164 | tf_op jit(solution)/shard_map/dot_general | solution.py:21
  85.8 3.2 %fusion.58 = f32[4,256,512]{2,1,0:T(8,128)} fusion(f32[4,256]{1,0:T(4,128)S(1)} %add_rsqrt_fusion.3, f32[512]{0:T(512)S(1)} %bitcast.190, bf16[4,3,512,512]{3,2,1,0:T(8,128)(2,1)} %all-gather.4.cloned.1.call-done, bf16[4,256,512]{2,1,0:T(8,128)(2,1)S(1)} %gather_fusion.1, pred[4]{0:T(512)(128)(4,1)S(1)} %get-tuple-element.203), kind=kOutput, calls=%fused_computation.106 | convolution fusion | flops 539492352 | bytes 3676164 | tf_op jit(solution)/shard_map/dot_general | solution.py:21
  89.0 30.7 %all-gather.6.cloned.1.call-done = bf16[4,512,512]{2,1,0:T(8,128)(2,1)} async-done(((bf16[1,512,512]{2,1,0:T(8,128)(2,1)}), bf16[4,512,512]{2,1,0:T(8,128)(2,1)}) %all-gather.6.cloned.1.call-update) | async-done | bytes 2097168 | tf_op jit(solution)/shard_map/all_gather | solution.py:92
  119.7 4.6 %fusion.24 = (f32[4,256]{1,0:T(4,128)S(1)}, bf16[4,256,512]{2,1,0:T(8,128)(2,1)}) fusion(bf16[4,512,512]{2,1,0:T(8,128)(2,1)} %all-gather.6.cloned.1.call-done, f32[4,256,512]{2,1,0:T(8,128)} %fusion.58, f32[4,256,512]{2,1,0:T(8,128)} %fusion.60, f32[4,256]{1,0:T(4,128)S(1)} %add_rsqrt_fusion.3, f32[512]{0:T(512)S(1)} %bitcast.191, ...), kind=kOutput, calls=%fused_computation.62 | convolution fusion | flops 1083702272 | bytes 8399872 | tf_op jit(solution)/shard_map/dot_general | solution.py:27
  124.3 3.5 %fusion.54 = f32[4,256,512]{2,1,0:T(8,128)} fusion(bf16[4,256,512]{2,1,0:T(8,128)(2,1)} %get-tuple-element.188, f32[4,256]{1,0:T(4,128)S(1)} %add_rsqrt_fusion.2, f32[512]{0:T(512)S(1)} %bitcast.183, bf16[4,3,512,512]{3,2,1,0:T(8,128)(2,1)} %all-gather.4.cloned.1.call-done), kind=kOutput, calls=%fused_computation.105 | convolution fusion | flops 538968064 | bytes 3676160 | tf_op jit(solution)/shard_map/dot_general | solution.py:21
  127.9 3.2 %fusion.52 = f32[4,256,512]{2,1,0:T(8,128)} fusion(bf16[4,256,512]{2,1,0:T(8,128)(2,1)S(1)} %copy-done.16, f32[4,256]{1,0:T(4,128)S(1)} %add_rsqrt_fusion.2, f32[512]{0:T(512)S(1)} %bitcast.184, bf16[4,3,512,512]{3,2,1,0:T(8,128)(2,1)} %all-gather.4.cloned.1.call-done), kind=kOutput, calls=%fused_computation.104 | convolution fusion | flops 538968064 | bytes 3676160 | tf_op jit(solution)/shard_map/dot_general | solution.py:21
  131.1 5.2 %fusion.27 = bf16[4,256,512]{2,1,0:T(8,128)(2,1)} fusion(bf16[4,256,512]{2,1,0:T(8,128)(2,1)} %get-tuple-element.188, f32[4,256,512]{2,1,0:T(8,128)} %fusion.52, f32[4,256,512]{2,1,0:T(8,128)} %fusion.54, f32[4,256]{1,0:T(4,128)S(1)} %add_rsqrt_fusion.2, f32[512]{0:T(512)S(1)} %bitcast.185, bf16[4,3,512,512]{3,2,1,0:T(8,128)(2,1)} %all-gather.4.cloned.1.call-done, ...), kind=kOutput, calls=%fused_computation.65 | convolution fusion | flops 1081081856 | bytes 8394752 | tf_op jit(solution)/shard_map/dot_general | solution.py:27
  136.2 2.4 fusion.131
  139.3 3.2 %fusion.104 = f32[4,256,512]{2,1,0:T(8,128)} fusion(f32[512]{0:T(512)S(1)} %bitcast.192, f32[4,256]{1,0:T(4,128)S(1)} %add_rsqrt_fusion.7, bf16[4,3,512,512]{3,2,1,0:T(8,128)(2,1)} %all-gather.4.cloned.1.call-done, bf16[4,256,512]{2,1,0:T(8,128)(2,1)S(1)} %gather_fusion, pred[4]{0:T(512)(128)(4,1)S(1)} %get-tuple-element.204), kind=kOutput, calls=%fused_computation.135 | convolution fusion | flops 539492352 | bytes 3676164 | tf_op jit(solution)/shard_map/dot_general | solution.py:21
  142.5 3.1 %fusion.106 = f32[4,256,512]{2,1,0:T(8,128)} fusion(f32[512]{0:T(512)S(1)} %bitcast.193, f32[4,256]{1,0:T(4,128)S(1)} %add_rsqrt_fusion.7, bf16[4,3,512,512]{3,2,1,0:T(8,128)(2,1)} %all-gather.4.cloned.1.call-done, bf16[4,256,512]{2,1,0:T(8,128)(2,1)S(1)} %gather_fusion, pred[4]{0:T(512)(128)(4,1)S(1)} %get-tuple-element.204), kind=kOutput, calls=%fused_computation.136 | convolution fusion | flops 539492352 | bytes 3676164 | tf_op jit(solution)/shard_map/dot_general | solution.py:21
  145.6 4.6 %fusion.16 = (f32[4,256]{1,0:T(4,128)S(1)}, bf16[4,256,512]{2,1,0:T(8,128)(2,1)}) fusion(bf16[4,512,512]{2,1,0:T(8,128)(2,1)} %all-gather.6.cloned.1.call-done, f32[4,256,512]{2,1,0:T(8,128)} %fusion.104, f32[4,256,512]{2,1,0:T(8,128)} %fusion.106, f32[512]{0:T(512)S(1)} %bitcast.194, f32[4,256]{1,0:T(4,128)S(1)} %add_rsqrt_fusion.7, ...), kind=kOutput, calls=%fused_computation.54 | convolution fusion | flops 1083702272 | bytes 8399872 | tf_op jit(solution)/shard_map/dot_general | solution.py:27
  150.2 3.6 %fusion.82 = f32[4,256,512]{2,1,0:T(8,128)} fusion(bf16[4,256,512]{2,1,0:T(8,128)(2,1)} %get-tuple-element.190, f32[512]{0:T(512)S(1)} %bitcast.186, f32[4,256]{1,0:T(4,128)S(1)} %add_rsqrt_fusion.6, bf16[4,3,512,512]{3,2,1,0:T(8,128)(2,1)} %all-gather.4.cloned.1.call-done), kind=kOutput, calls=%fused_computation.119 | convolution fusion | flops 538968064 | bytes 3676160 | tf_op jit(solution)/shard_map/dot_general | solution.py:21
  153.8 3.1 %fusion.84 = f32[4,256,512]{2,1,0:T(8,128)} fusion(bf16[4,256,512]{2,1,0:T(8,128)(2,1)S(1)} %copy-done.15, f32[512]{0:T(512)S(1)} %bitcast.187, f32[4,256]{1,0:T(4,128)S(1)} %add_rsqrt_fusion.6, bf16[4,3,512,512]{3,2,1,0:T(8,128)(2,1)} %all-gather.4.cloned.1.call-done), kind=kOutput, calls=%fused_computation.120 | convolution fusion | flops 538968064 | bytes 3676160 | tf_op jit(solution)/shard_map/dot_general | solution.py:21
  156.9 4.3 %fusion.19 = bf16[4,256,512]{2,1,0:T(8,128)(2,1)S(1)} fusion(bf16[4,256,512]{2,1,0:T(8,128)(2,1)} %get-tuple-element.190, f32[4,256,512]{2,1,0:T(8,128)} %fusion.82, f32[4,256,512]{2,1,0:T(8,128)} %fusion.84, f32[512]{0:T(512)S(1)} %bitcast.188, f32[4,256]{1,0:T(4,128)S(1)} %add_rsqrt_fusion.6, bf16[4,3,512,512]{3,2,1,0:T(8,128)(2,1)} %all-gather.4.cloned.1.call-done, ...), kind=kOutput, calls=%fused_computation.57 | convolution fusion | flops 1081081856 | bytes 8394752 | tf_op jit(solution)/shard_map/dot_general | solution.py:27
  161.3 1.1 fusion.125
  164.6 39.3 %all-reduce.16 = (f32[8,18]{1,0:T(8,128)S(1)}, f32[8]{0:T(128)S(1)}) all-reduce(f32[8,18]{1,0:T(8,128)S(1)} %scatter-add.19, f32[8]{0:T(128)S(1)} %fusion.155), channel_id=1, replica_groups=mesh['section'=4,'dp'=8] {'section','dp'}, use_global_device_ids=true, to_apply=%region_18.20 | all-reduce | flops 152 | bytes 1216 | tf_op jit(solution)/shard_map/psum | solution.py:110
  212.2 3.1 %fusion.120 = f32[4,256,512]{2,1,0:T(8,128)} fusion(bf16[4,256,512]{2,1,0:T(8,128)(2,1)S(1)} %bitcast.170, bf16[4,3,512,512]{3,2,1,0:T(8,128)(2,1)} %all-gather.4.cloned.1.call-done), kind=kOutput, calls=%fused_computation.160 | convolution fusion | flops 536870912 | bytes 3670016 | tf_op jit(solution)/shard_map/dot_general | solution.py:21
  215.3 3.1 %fusion.118 = f32[4,256,512]{2,1,0:T(8,128)} fusion(bf16[4,256,512]{2,1,0:T(8,128)(2,1)S(1)} %bitcast.171, bf16[4,3,512,512]{3,2,1,0:T(8,128)(2,1)} %all-gather.4.cloned.1.call-done), kind=kOutput, calls=%fused_computation.158 | convolution fusion | flops 536870912 | bytes 3670016 | tf_op jit(solution)/shard_map/dot_general | solution.py:21
  218.4 5.2 %fusion.28 = (f32[4,256]{1,0:T(4,128)S(1)}, bf16[4,256,512]{2,1,0:T(8,128)(2,1)}) fusion(f32[4,256,512]{2,1,0:T(8,128)} %bitcast.174, bf16[4,512,512]{2,1,0:T(8,128)(2,1)} %all-gather.6.cloned.1.call-done, f32[4,256,512]{2,1,0:T(8,128)} %fusion.120, f32[4,256,512]{2,1,0:T(8,128)} %fusion.118, bf16[4,256,512]{2,1,0:T(8,128)(2,1)S(1)} %bitcast.172, ...), kind=kOutput, calls=%fused_computation.66 | convolution fusion | flops 1080032256 | bytes 9441280 | tf_op jit(solution)/shard_map/dot_general | solution.py:27
  223.6 3.5 %fusion.48 = f32[4,256,512]{2,1,0:T(8,128)} fusion(bf16[4,256,512]{2,1,0:T(8,128)(2,1)} %get-tuple-element.196, f32[4,256]{1,0:T(4,128)S(1)} %add_rsqrt_fusion, f32[512]{0:T(512)S(1)} %bitcast.177, bf16[4,3,512,512]{3,2,1,0:T(8,128)(2,1)} %all-gather.4.cloned.1.call-done), kind=kOutput, calls=%fused_computation.103 | convolution fusion | flops 538968064 | bytes 3676160 | tf_op jit(solution)/shard_map/dot_general | solution.py:21
  227.1 3.2 %fusion.46 = f32[4,256,512]{2,1,0:T(8,128)} fusion(bf16[4,256,512]{2,1,0:T(8,128)(2,1)S(1)} %copy-done.14, f32[4,256]{1,0:T(4,128)S(1)} %add_rsqrt_fusion, f32[512]{0:T(512)S(1)} %bitcast.178, bf16[4,3,512,512]{3,2,1,0:T(8,128)(2,1)} %all-gather.4.cloned.1.call-done), kind=kOutput, calls=%fused_computation.102 | convolution fusion | flops 538968064 | bytes 3676160 | tf_op jit(solution)/shard_map/dot_general | solution.py:21
  230.3 3.8 %fusion.43 = f32[4,256]{1,0:T(4,128)S(1)} fusion(f32[4,256,512]{2,1,0:T(8,128)} %fusion.46, f32[4,256,512]{2,1,0:T(8,128)} %fusion.48, bf16[4,256,512]{2,1,0:T(8,128)(2,1)S(1)} %copy-done.14, f32[4,256]{1,0:T(4,128)S(1)} %add_rsqrt_fusion, f32[512]{0:T(512)S(1)} %bitcast.179, bf16[4,3,512,512]{3,2,1,0:T(8,128)(2,1)} %all-gather.4.cloned.1.call-done, ...), kind=kOutput, calls=%fused_computation.81 | convolution fusion | flops 1084226560 | bytes 8399360 | tf_op jit(solution)/shard_map/dot_general | solution.py:27
  234.0 3.0 %fusion.121 = f32[4,256,512]{2,1,0:T(8,128)} fusion(bf16[4,256,512]{2,1,0:T(8,128)(2,1)S(1)} %bitcast.167, bf16[4,3,512,512]{3,2,1,0:T(8,128)(2,1)} %all-gather.4.cloned.1.call-done), kind=kOutput, calls=%fused_computation.161 | convolution fusion | flops 536870912 | bytes 3670016 | tf_op jit(solution)/shard_map/dot_general | solution.py:21
  237.1 3.3 %fusion.119 = f32[4,256,512]{2,1,0:T(8,128)} fusion(bf16[4,256,512]{2,1,0:T(8,128)(2,1)S(1)} %bitcast.168, bf16[4,3,512,512]{3,2,1,0:T(8,128)(2,1)} %all-gather.4.cloned.1.call-done), kind=kOutput, calls=%fused_computation.159 | convolution fusion | flops 536870912 | bytes 3670016 | tf_op jit(solution)/shard_map/dot_general | solution.py:21
  240.3 4.4 %fusion.20 = (f32[4,256]{1,0:T(4,128)S(1)}, bf16[4,256,512]{2,1,0:T(8,128)(2,1)}) fusion(f32[4,256,512]{2,1,0:T(8,128)S(1)} %bitcast.173, bf16[4,512,512]{2,1,0:T(8,128)(2,1)} %all-gather.6.cloned.1.call-done, f32[4,256,512]{2,1,0:T(8,128)} %fusion.121, f32[4,256,512]{2,1,0:T(8,128)} %fusion.119, bf16[4,256,512]{2,1,0:T(8,128)(2,1)S(1)} %bitcast.169, ...), kind=kOutput, calls=%fused_computation.58 | convolution fusion | flops 1080032256 | bytes 9441280 | tf_op jit(solution)/shard_map/dot_general | solution.py:27
  244.7 3.6 %fusion.68 = f32[4,256,512]{2,1,0:T(8,128)} fusion(bf16[4,256,512]{2,1,0:T(8,128)(2,1)} %get-tuple-element.198, f32[512]{0:T(512)S(1)} %bitcast.180, f32[4,256]{1,0:T(4,128)S(1)} %add_rsqrt_fusion.4, bf16[4,3,512,512]{3,2,1,0:T(8,128)(2,1)} %all-gather.4.cloned.1.call-done), kind=kOutput, calls=%fused_computation.111 | convolution fusion | flops 538968064 | bytes 3676160 | tf_op jit(solution)/shard_map/dot_general | solution.py:21
  248.4 3.2 %fusion.70 = f32[4,256,512]{2,1,0:T(8,128)} fusion(bf16[4,256,512]{2,1,0:T(8,128)(2,1)S(1)} %copy-done.13, f32[512]{0:T(512)S(1)} %bitcast.181, f32[4,256]{1,0:T(4,128)S(1)} %add_rsqrt_fusion.4, bf16[4,3,512,512]{3,2,1,0:T(8,128)(2,1)} %all-gather.4.cloned.1.call-done), kind=kOutput, calls=%fused_computation.112 | convolution fusion | flops 538968064 | bytes 3676160 | tf_op jit(solution)/shard_map/dot_general | solution.py:21
  251.6 3.8 %fusion.37 = f32[4,256]{1,0:T(4,128)S(1)} fusion(f32[4,256,512]{2,1,0:T(8,128)} %fusion.68, f32[4,256,512]{2,1,0:T(8,128)} %fusion.70, bf16[4,256,512]{2,1,0:T(8,128)(2,1)S(1)} %copy-done.13, f32[512]{0:T(512)S(1)} %bitcast.182, f32[4,256]{1,0:T(4,128)S(1)} %add_rsqrt_fusion.4, bf16[4,3,512,512]{3,2,1,0:T(8,128)(2,1)} %all-gather.4.cloned.1.call-done, ...), kind=kOutput, calls=%fused_computation.75 | convolution fusion | flops 1084226560 | bytes 8399360 | tf_op jit(solution)/shard_map/dot_general | solution.py:27
  (91 shorter events, 15.9 us)
Async XLA Ops:
  7.2 202.5 %copy-start = (bf16[18,512]{1,0:T(8,128)(2,1)S(1)}, bf16[18,512]{1,0:T(8,128)(2,1)}, u32[]{:S(2)}) copy-start(bf16[18,512]{1,0:T(8,128)(2,1)} %param.43) | copy-start | bytes 55300
  7.2 1.5 copy-start.7
  7.2 12.6 %copy-start.8 = (s32[8,4]{0,1:T(4,128)S(1)}, s32[8,4]{0,1:T(4,128)}, u32[]{:S(2)}) copy-start(s32[8,4]{0,1:T(4,128)} %param.36) | copy-start | bytes 388
  7.2 75.5 %all-gather.4.cloned.1.call-start = ((), (), s32[]{:S(2)}) async-start(), calls=%async_computation | async-start | bytes 7864320 | tf_op jit(solution)/shard_map/all_gather | solution.py:91
  7.9 111.8 %all-gather.6.cloned.1.call-start = ((), (), s32[]{:S(2)}) async-start(), calls=%async_computation.1 | async-start | bytes 2621440 | tf_op jit(solution)/shard_map/all_gather | solution.py:92
  20.1 14.6 %copy-start.10 = (bf16[1,512]{1,0:T(2,128)(2,1)S(1)}, bf16[1,512]{1,0:T(2,128)(2,1)}, u32[]{:S(2)}) copy-start(bf16[1,512]{1,0:T(2,128)(2,1)} %param.40) | copy-start | bytes 3076
  20.1 23.9 %copy-start.9 = (s32[2]{0:T(128)S(1)}, s32[2]{0:T(128)}, u32[]{:S(2)}) copy-start(s32[2]{0:T(128)} %constant.321.clone.1) | copy-start | bytes 28
  25.0 120.6 %copy-start.5 = (bf16[4,256,512]{2,1,0:T(8,128)(2,1)}, bf16[4,256,512]{2,1,0:T(8,128)(2,1)S(1)}, u32[]{:S(2)}) copy-start(bf16[4,256,512]{2,1,0:T(8,128)(2,1)S(1)} %gather_fusion) | copy-start | bytes 3145732
  124.3 3.5 %copy-start.16 = (bf16[4,256,512]{2,1,0:T(8,128)(2,1)S(1)}, bf16[4,256,512]{2,1,0:T(8,128)(2,1)}, u32[]{:S(2)}) copy-start(bf16[4,256,512]{2,1,0:T(8,128)(2,1)} %get-tuple-element.188) | copy-start | bytes 3145732
  131.1 5.2 %copy-start.11 = (bf16[512,18]{0,1:T(8,128)(2,1)S(1)}, bf16[512,18]{0,1:T(8,128)(2,1)}, u32[]{:S(2)}) copy-start(bf16[512,18]{0,1:T(8,128)(2,1)} %param.41) | copy-start | bytes 55300
  131.1 5.2 %copy-start.12 = (f32[18]{0:T(128)S(1)}, f32[18]{0:T(128)}, u32[]{:S(2)}) copy-start(f32[18]{0:T(128)} %param.42) | copy-start | bytes 220
  150.2 3.6 %copy-start.15 = (bf16[4,256,512]{2,1,0:T(8,128)(2,1)S(1)}, bf16[4,256,512]{2,1,0:T(8,128)(2,1)}, u32[]{:S(2)}) copy-start(bf16[4,256,512]{2,1,0:T(8,128)(2,1)} %get-tuple-element.190) | copy-start | bytes 3145732
  210.2 1.4 copy-start.2
  210.8 1.4 copy-start.4
  223.6 3.5 %copy-start.14 = (bf16[4,256,512]{2,1,0:T(8,128)(2,1)S(1)}, bf16[4,256,512]{2,1,0:T(8,128)(2,1)}, u32[]{:S(2)}) copy-start(bf16[4,256,512]{2,1,0:T(8,128)(2,1)} %get-tuple-element.196) | copy-start | bytes 3145732
  237.1 3.3 %copy-start.3 = (f32[1024,512]{1,0:T(8,128)S(1)}, f32[1024,512]{1,0:T(8,128)}, u32[]{:S(2)}) copy-start(f32[1024,512]{1,0:T(8,128)} %copy-done.2) | copy-start | bytes 6291460
  244.7 3.6 %copy-start.13 = (bf16[4,256,512]{2,1,0:T(8,128)(2,1)S(1)}, bf16[4,256,512]{2,1,0:T(8,128)(2,1)}, u32[]{:S(2)}) copy-start(bf16[4,256,512]{2,1,0:T(8,128)(2,1)} %get-tuple-element.198) | copy-start | bytes 3145732
  248.4 3.2 %copy-start.6 = (bf16[4,256,512]{2,1,0:T(8,128)(2,1)S(1)}, bf16[4,256,512]{2,1,0:T(8,128)(2,1)}, u32[]{:S(2)}) copy-start(bf16[4,256,512]{2,1,0:T(8,128)(2,1)} %copy-done.5) | copy-start | bytes 3145732
  251.5 4.9 %copy-start.1 = (bf16[18,512]{1,0:T(8,128)(2,1)S(1)}, bf16[18,512]{1,0:T(8,128)(2,1)}, u32[]{:S(2)}) copy-start(bf16[18,512]{1,0:T(8,128)(2,1)} %param.43) | copy-start | bytes 55300
Sparse Core Ops, SparseCore 0:
  9.9 72.7 all-gather.3
  84.5 35.1 all-gather.5
where the time goes:
time: 265 us; the launch traced here: 263 us
  matrix products  92.5 us (35%)
  waiting for transfers between devices  68.2 us (26%)
  blocking collectives  48.6 us (18%)
  between operations  31.2 us (12%)
  local copies, waits for them, and re-layouts  11.6 us (4%)
  other arithmetic  11.1 us (4%)
    dot_general x16, matrix products, run_block(): jnp.dot(flat, tap_set[k], preferred_element_type=jnp.float32)  52 us
    psum x1, blocking collectives, on_device(): lax.psum((bit_buffer, entropy_buffer), ('section', 'dp'))  39.3 us
    all_gather x1, waiting for transfers between devices, on_device(): lax.all_gather(tap_weights, 'section', axis=0, tiled=True)  36.1 us
    dot_general x8, matrix products, run_block(): jnp.dot(activated.reshape(-1, channels), out_weight, preferred_element_ty...  35.9 us
    all_gather x1, waiting for transfers between devices, on_device(): lax.all_gather(out_weights, 'section', axis=0, tiled=True)  30.7 us
    all_gather x1, blocking collectives, on_device(): lax.all_gather(norm_gains, 'section', axis=0, tiled=True)  9.32 us
    gather x2, local copies, waits for them, and re-layouts, on_device(): source = jnp.take(clip_pool, clip_index[batch_slot], axis=0)  9.28 us
    another operation x12, other arithmetic  8.18 us
  transfers between devices with their start and end apart: 2, of which 2 were waited for; matrix products, arithmetic and copies ran while one was open for 7% of the time, Pallas kernels for 0%

commit v1 on v0

v1 whole, which is shorter than its diff:
```python
import functools

import jax
import jax.numpy as jnp
from jax import lax
from jax.experimental import pallas as pl
from jax.experimental.pallas import tpu as pltpu
from jax.sharding import PartitionSpec as P

MESH = pl.DeviceIdType.MESH
SPATIAL = 64
norm_eps = 1e-06
quant_section = 1


def kernel(
    sections,
    dps,
    idx_ref,
    order_ref,
    pool_ref,
    taps_ref,
    out_w_ref,
    gain_ref,
    qw_ref,
    qb_ref,
    pw_ref,
    err_ref,
    loss_ref,
    pool,
    weights,
    gains,
    source,
    current,
    normed,
    stat_dp,
    stat_all,
    pool_sem,
    own_sem,
    a_send,
    a_recv,
    g_send,
    g_recv,
    core_send,
    core_recv,
    chip_send,
    chip_recv,
    dp_send,
    dp_recv,
    all_send,
    all_recv,
):
    s = lax.axis_index("section")
    d = lax.axis_index("dp")
    taps, chan = taps_ref.shape[1], taps_ref.shape[2]
    mats = taps + 1
    per_section, clips = err_ref.shape[0], err_ref.shape[1]
    rows = err_ref.shape[2]
    frames = rows // SPATIAL
    group = per_section * clips * SPATIAL
    half = clips * SPATIAL
    bits = qw_ref.shape[1]
    batches = per_section * sections

    q = d % mats
    core_peer = d + 1 - 2 * (d % 2)
    chip_peer = d + 2 - 4 * ((d // 2) % 2)
    q_chip = chip_peer % mats
    q_core = core_peer % mats
    q_far = (chip_peer + 1 - 2 * (chip_peer % 2)) % mats

    pool_copy = pltpu.make_async_copy(pool_ref, pool, pool_sem)
    own_taps = [
        pltpu.make_async_copy(
            taps_ref.at[0, k], weights.at[s, pl.ds(k * chan, chan)], own_sem.at[k]
        )
        for k in range(taps)
    ]
    own_out = pltpu.make_async_copy(
        out_w_ref.at[0], weights.at[s, pl.ds(taps * chan, chan)], own_sem.at[taps]
    )
    for c in own_taps:
        c.start()
    own_out.start()
    pool_copy.start()
    gains[s] = gain_ref[...].astype(jnp.float32)

    barrier = pltpu.get_barrier_semaphore()
    for k in range(1, sections):
        pl.semaphore_signal(barrier, inc=1, device_id=((s + k) % sections, d), device_id_type=MESH)
    for k in range(1, dps):
        pl.semaphore_signal(barrier, inc=1, device_id=(s, (d + k) % dps), device_id_type=MESH)
    for c in own_taps:
        c.wait()
    own_out.wait()
    pl.semaphore_wait(barrier, sections - 1 + dps - 1)

    def part(b, p):
        return weights.at[b, pl.ds(pl.multiple_of(p * chan, chan), chan)]

    def remote(ref, send, recv, to):
        return pltpu.make_async_remote_copy(
            src_ref=ref, dst_ref=ref, send_sem=send, recv_sem=recv, device_id=to, device_id_type=MESH
        )

    def direct(b, slot, to):
        return remote(part(b, q), a_send.at[slot], a_recv.at[b], to)

    def gain_copy(b, slot, to):
        return remote(gains.at[b], g_send.at[slot], g_recv.at[b], to)

    def to_core(b, p, slot):
        return remote(part(b, p), core_send.at[b, slot], core_recv.at[b, slot], (s, core_peer))

    def to_chip(b, p):
        return remote(part(b, p), chip_send.at[b], chip_recv.at[b], (s, chip_peer))

    for k in range(1, sections):
        direct(s, k - 1, ((s + k) % sections, d)).start()
    for k in range(1, sections):
        gain_copy(s, k - 1, ((s + k) % sections, d)).start()

    def step1(b):
        @pl.when(s != b)
        def _():
            direct(b, 0, (s, d)).wait_recv()
            to_chip(b, q).start()
            to_core(b, q, 0).start()

    def step2(b):
        @pl.when(s != b)
        def _():
            to_chip(b, q_chip).wait_recv()
            to_core(b, q_chip, 1).start()

    def step3(b):
        @pl.when(s != b)
        def _():
            gain_copy(b, 0, (s, d)).wait_recv()
            to_core(b, q_core, 0).wait_recv()
            to_core(b, q_far, 1).wait_recv()

    pool_copy.wait()
    for i in range(per_section):
        for c in range(clips):
            clip = idx_ref[s * per_section + i, c]
            for f in range(frames):
                start = f * group + (i * clips + c) * SPATIAL
                piece = pool[clip, f * SPATIAL : (f + 1) * SPATIAL, :]
                source[start : start + SPATIAL, :] = piece

    def norm(b, f, src):
        v = src[f * group : (f + 1) * group, :].astype(jnp.float32)
        scale = lax.rsqrt(jnp.mean(v * v, axis=-1, keepdims=True) + norm_eps)
        normed[f * group : (f + 1) * group, :] = (v * scale * gains[b]).astype(jnp.bfloat16)

    def block(b, f, src):
        depth = min(f + 1, taps)
        left = [normed[(f - k) * group : (f - k + 1) * group, :] for k in range(depth)]
        left = jnp.concatenate(left, axis=1) if depth > 1 else left[0]
        mixed = jnp.dot(left, weights[b, 0 : depth * chan, :], preferred_element_type=jnp.float32)
        bent = 0.5 * mixed
        activated = (bent * jnp.tanh(bent) + bent).astype(jnp.bfloat16)
        update = jnp.dot(
            activated, weights[b, taps * chan : mats * chan, :], preferred_element_type=jnp.float32
        )
        return (src[f * group : (f + 1) * group, :].astype(jnp.float32) + update).astype(jnp.bfloat16)

    sums = [None] * per_section

    def quantize(v):
        logits = jnp.dot(v, qw_ref[...], preferred_element_type=jnp.float32) + qb_ref[...]
        x = 4.0 * logits
        size = jnp.abs(x)
        e = jnp.exp(-size)
        low = e / (1.0 + e)
        prob = jnp.where(x >= 0, 1.0 - low, low)
        entropy = jnp.log1p(e) + size * low
        for i in range(per_section):
            bit = jnp.sum(prob[i * half : (i + 1) * half], axis=0, keepdims=True)
            ent = jnp.sum(entropy[i * half : (i + 1) * half], axis=0, keepdims=True)
            sums[i] = (bit, ent) if sums[i] is None else (sums[i][0] + bit, sums[i][1] + ent)
        codes = (2.0 * prob - 1.0).astype(jnp.bfloat16)
        return jnp.dot(codes, pw_ref[...], preferred_element_type=jnp.float32).astype(jnp.bfloat16)

    def put_error(f, v):
        differ = v.astype(jnp.float32) - source[f * group : (f + 1) * group, :].astype(jnp.float32)
        return jnp.mean(differ * differ, axis=-1, keepdims=True)

    def dp_copy(slot, to):
        return remote(stat_dp.at[slot[0]], dp_send.at[slot[1]], dp_recv.at[slot[0]], to)

    def all_copy(slot, to):
        return remote(stat_all.at[slot[0]], all_send.at[slot[1]], all_recv.at[slot[0]], to)

    def send_dp():
        for k in range(1, dps):
            dp_copy((d, k - 1), (s, (d + k) % dps)).start()

    def send_all():
        for k in range(1, dps):
            dp_copy(((d + k) % dps, 0), (s, d)).wait_recv()
        total = stat_dp[0]
        for k in range(1, dps):
            total = total + stat_dp[k]
        stat_all[s] = total

    def start_all():
        for k in range(1, sections):
            all_copy((s, k - 1), ((s + k) % sections, d)).start()

    def finish():
        for k in range(1, sections):
            all_copy(((s + k) % sections, 0), (s, d)).wait_recv()
        stats = jnp.concatenate([stat_all[k] for k in range(sections)], axis=0)
        rows_total = float(clips * dps * rows)
        marginal = stats / rows_total
        lane = lax.broadcasted_iota(jnp.int32, marginal.shape, 1)
        row = lax.broadcasted_iota(jnp.int32, marginal.shape, 0)
        averaged = jnp.zeros_like(marginal)
        running = None
        for t in range(batches):
            at = row == order_ref[t]
            here = jnp.sum(jnp.where(at, marginal, 0.0), axis=0, keepdims=True)
            running = here if t == 0 else 0.5 * running + 0.5 * here
            averaged = jnp.where(at, running, averaged)
        smoothed = jnp.where(lane < bits, 0.05 + 0.9 * averaged, 0.5)
        term = smoothed * jnp.log(smoothed) + (1.0 - smoothed) * jnp.log(1.0 - smoothed)
        is_entropy = (lane >= bits) & (lane < 2 * bits)
        term = jnp.where(lane < bits, term, jnp.where(is_entropy, marginal, 0.0))
        loss = jnp.sum(term, axis=-1, keepdims=True)
        wide = lax.broadcasted_iota(jnp.int32, (batches, batches), 1)
        tall = lax.broadcasted_iota(jnp.int32, (batches, batches), 0)
        loss_ref[...] = jnp.sum(jnp.where(wide == tall, loss, 0.0), axis=0, keepdims=True)

    hooks = {
        (0, 0): lambda: step2(1),
        (0, 1): lambda: step1(2),
        (0, 2): lambda: step1(3),
        (0, 3): lambda: (step2(2), step3(1)),
        (1, 0): lambda: step2(3),
        (1, 3): lambda: step3(2),
        (2, 0): send_dp,
        (2, 2): send_all,
        (2, 3): lambda: (start_all(), step3(3)),
    }
    step1(0)
    step1(1)
    step2(0)
    step3(0)
    errors = []
    for b in range(sections):
        src = source if b == 0 else current
        for f in range(frames):
            norm(b, f, src)
        for f in range(frames):
            v = block(b, f, src)
            if b == quant_section:
                v = quantize(v)
            if b == sections - 1:
                errors.append(put_error(f, v))
            else:
                current[f * group : (f + 1) * group, :] = v
            if b == quant_section and f == frames - 1:
                stat_dp[d] = jnp.zeros(stat_dp.shape[1:], jnp.float32)
                for i in range(per_section):
                    stat_dp[d, i : i + 1, 0:bits] = sums[i][0]
                    stat_dp[d, i : i + 1, bits : 2 * bits] = sums[i][1]
            if (b, f) in hooks:
                hooks[(b, f)]()

    wide = lax.broadcasted_iota(jnp.int32, (2 * SPATIAL, 2 * SPATIAL), 1)
    tall = lax.broadcasted_iota(jnp.int32, (2 * SPATIAL, 2 * SPATIAL), 0)
    for i in range(per_section):
        for c in range(clips):
            at = (i * clips + c) * SPATIAL
            for g in range(frames // 2):
                column = jnp.concatenate(
                    [errors[2 * g + h][at : at + SPATIAL] for h in range(2)], axis=0
                )
                line = jnp.sum(jnp.where(wide == tall, column, 0.0), axis=0, keepdims=True)
                err_ref[i, c : c + 1, g * 2 * SPATIAL : (g + 1) * 2 * SPATIAL] = line
    finish()

    for k in range(1, sections):
        to = ((s + k) % sections, d)
        direct(s, k - 1, to).wait_send()
        gain_copy(s, k - 1, to).wait_send()
        all_copy((s, k - 1), to).wait_send()
    for k in range(1, dps):
        dp_copy((d, k - 1), (s, (d + k) % dps)).wait_send()
    for b in range(sections):

        @pl.when(s != b)
        def _():
            to_chip(b, q).wait_send()
            to_core(b, q, 0).wait_send()
            to_core(b, q_chip, 1).wait_send()


def solution(mesh):
    sections, dps = mesh.shape["section"], mesh.shape["dp"]

    def on_device(pool, index, order, taps, out_w, gain, qw, qb, pw):
        batches, clips = index.shape
        per_section = batches // sections
        held, rows, chan = pool.shape
        mats = taps.shape[1] + 1
        flat = per_section * clips * rows
        vmem = pl.BlockSpec(memory_space=pltpu.VMEM)
        smem = pl.BlockSpec(memory_space=pltpu.SMEM)
        hbm = pl.BlockSpec(memory_space=pl.ANY)
        dma = pltpu.SemaphoreType.DMA
        err, loss = pl.pallas_call(
            functools.partial(kernel, sections, dps),
            out_shape=(
                jax.ShapeDtypeStruct((per_section, clips, rows), jnp.float32),
                jax.ShapeDtypeStruct((1, batches), jnp.float32),
            ),
            in_specs=[smem, smem, hbm, hbm, hbm, vmem, vmem, vmem, vmem],
            out_specs=(vmem, vmem),
            scratch_shapes=[
                pltpu.VMEM((held, rows, chan), jnp.bfloat16),
                pltpu.VMEM((sections, mats * chan, chan), jnp.bfloat16),
                pltpu.VMEM((sections, 1, chan), jnp.float32),
                pltpu.VMEM((flat, chan), jnp.bfloat16),
                pltpu.VMEM((flat, chan), jnp.bfloat16),
                pltpu.VMEM((flat, chan), jnp.bfloat16),
                pltpu.VMEM((dps, per_section, 128), jnp.float32),
                pltpu.VMEM((sections, per_section, 128), jnp.float32),
                dma,
                dma((mats,)),
                dma((sections - 1,)),
                dma((sections,)),
                dma((sections - 1,)),
                dma((sections,)),
                dma((sections, 2)),
                dma((sections, 2)),
                dma((sections,)),
                dma((sections,)),
                dma((dps - 1,)),
                dma((dps,)),
                dma((sections - 1,)),
                dma((sections,)),
            ],
            compiler_params=pltpu.CompilerParams(
                collective_id=0, has_side_effects=True, vmem_limit_bytes=60 * 1024 * 1024
            ),
        )(index, order, pool, taps, out_w, gain, qw, qb.reshape(1, -1), pw)
        return err, loss.reshape(batches)

    return jax.shard_map(
        on_device,
        mesh=mesh,
        in_specs=(
            P("dp", None, None),
            P(None, "dp"),
            P(),
            P("section", None, None, None),
            P("section", None, None),
            P("section", None),
            P(),
            P(),
            P(),
        ),
        out_specs=(P("section", "dp", None), P()),
        check_vma=False,
    )
```

time: 265 us -> 92.7 us (0.35)
  matrix products: 92.5 us -> 0 us
  Pallas kernels: 0 us -> 86.5 us
  waiting for transfers between devices: 68.2 us -> 0 us
  blocking collectives: 48.6 us -> 0 us
  between operations: 31.2 us -> 0.64 us
  other arithmetic: 11.1 us -> 0 us
  local copies, waits for them, and re-layouts: 11.6 us -> 5.32 us
    dot_general x28 -> x0, matrix products: 92.5 us -> none  [the longest x16 52 us: run_block(): jnp.dot(flat, tap_set[k], preferred_element_type=jnp.float32)]
    pallas_call x0 -> x1, Pallas kernels: none -> 86.5 us  [on_device(): pl.pallas_call(functools.partial(kernel, sections, dps), out_shape=(jax.S...]
    all_gather x2 -> x0, waiting for transfers between devices: 66.8 us -> none  [the longest x1 36.1 us: on_device(): lax.all_gather(tap_weights, 'section', axis=0, tiled=True)]
    psum x1 -> x0, blocking collectives: 39.3 us -> none  [on_device(): lax.psum((bit_buffer, entropy_buffer), ('section', 'dp'))]
    all_gather x1 -> x0, blocking collectives: 9.32 us -> none  [on_device(): lax.all_gather(norm_gains, 'section', axis=0, tiled=True)]
    gather x2 -> x0, local copies, waits for them, and re-layouts: 9.28 us -> none  [on_device(): source = jnp.take(clip_pool, clip_index[batch_slot], axis=0)]
    another operation x13 -> x0, other arithmetic: 8.79 us -> none
    unnamed x34 -> x4, local copies, waits for them, and re-layouts: 1.01 us -> 5.32 us
  transfers between devices with their start and end apart: 2 -> 0, of which waited for: 2 -> 0; matrix products, arithmetic and copies ran while one was open for 7% -> 0% of each run, Pallas kernels for 0% -> 0%
where the time goes in v1:
time: 92.7 us; the launch traced here: 92.5 us
  Pallas kernels  86.5 us (93%)
  local copies, waits for them, and re-layouts  5.32 us (6%)
    pallas_call x1, Pallas kernels, on_device(): pl.pallas_call(functools.partial(kernel, sections, dps), out_shape=(jax.S...  86.5 us
    unnamed x4, local copies, waits for them, and re-layouts  5.32 us

profile of v1, /device:TPU:0, one launch (start us, length us, event | category | flops | bytes accessed | tf_op | source)
XLA Modules:
  0.0 92.5 jit_solution(10934802210847199384)
XLA Ops:
  0.6 1.3 %copy.11.idx_ref = s32[8,4]{1,0:T(8,128)} copy(s32[8,4]{0,1:T(4,128)} %param.10) | data formatting | bytes 256 | tf_op args[1]
  2.0 1.5 %copy.12.qw_ref = bf16[512,18]{1,0:T(8,128)(2,1)} copy(bf16[512,18]{0,1:T(8,128)(2,1)} %param.15) | data formatting | bytes 36864 | tf_op args[6]
  3.5 86.5 %shard_map.104 = (f32[2,4,256]{2,1,0:T(4,128)}, f32[1,8]{1,0:T(1,128)}) custom-call(s32[8,4]{1,0:T(8,128)} %copy.11.idx_ref, s32[8]{0:T(128)} %order_ref.1, bf16[32,256,512]{2,1,0:T(8,128)(2,1)} %pool_ref.1, bf16[1,3,512,512]{3,2,1,0:T(8,128)(2,1)} %taps_ref.1, bf16[1,512,512]{2,1,0:T(8,128)(2,1)} %out_w_ref.1, bf16[1,512]{1,0:T(2,128)(2,1)} %gain_ref.1, ...), custom_call_target="tpu_custom_call" | custom-call | tf_op jit(solution)/shard_map/pallas_call | solution.py:314
  90.0 1.3 %copy.15 = f32[2,4,256]{2,1,0:T(4,128)} copy(f32[2,4,256]{2,1,0:T(4,128)} %get-tuple-element.8) | data formatting | bytes 16384
  91.3 1.2 %copy.16 = f32[8]{0:T(128)} copy(f32[8]{0:T(128)} %bitcast.3) | data formatting | bytes 64

commit v2 on v1

--- a/solution.py
+++ b/solution.py
@@ -39,6 +39,7 @@
     own_sem,
     a_send,
     a_recv,
+    r_send,
     g_send,
     g_recv,
     core_send,
@@ -59,7 +60,7 @@
     frames = rows // SPATIAL
     group = per_section * clips * SPATIAL
     half = clips * SPATIAL
-    bits = qw_ref.shape[1]
+    bits = qw_ref.shape[0]
     batches = per_section * sections
 
     q = d % mats
@@ -95,55 +96,151 @@
     own_out.wait()
     pl.semaphore_wait(barrier, sections - 1 + dps - 1)
 
-    def part(b, p):
-        return weights.at[b, pl.ds(pl.multiple_of(p * chan, chan), chan)]
+    sub = chan // mats
+    atoms = mats + mats // 2
+    shared = mats // 2
+    along_x = s + 1 - 2 * (s % 2)
+    along_y = s + 2 - 4 * ((s // 2) % 2)
+    diagonal = along_y + 1 - 2 * (along_y % 2)
+    even, odd = list(range(0, atoms, 2)), list(range(1, atoms, 2))
+    x_order, y_order = even + odd, odd + even
+
+    def place(first, second, j):
+        if j < mats:
+            return first, j
+        if j < atoms:
+            return second, j - shared
+        return second, j - atoms
+
+    def piece_of(b, first, second, j):
+        p, k = place(first, second, j)
+        return weights.at[b, pl.ds(pl.multiple_of(p * chan + k * sub, sub), sub)]
 
     def remote(ref, send, recv, to):
         return pltpu.make_async_remote_copy(
             src_ref=ref, dst_ref=ref, send_sem=send, recv_sem=recv, device_id=to, device_id_type=MESH
         )
 
-    def direct(b, slot, to):
-        return remote(part(b, q), a_send.at[slot], a_recv.at[b], to)
+    def atom(b, j, send, to):
+        return remote(piece_of(b, q, q_chip, j), send, a_recv.at[b, j], to)
+
+    def own_x(j):
+        return atom(s, j, a_send.at[0, j], (along_x, d))
+
+    def own_y(j):
+        return atom(s, j, a_send.at[1, j], (along_y, d))
+
+    def relay_x(i):
+        return atom(along_y, odd[i], r_send.at[0, i], (along_x, d))
+
+    def relay_y(i):
+        return atom(along_x, even[i], r_send.at[1, i], (along_y, d))
 
     def gain_copy(b, slot, to):
         return remote(gains.at[b], g_send.at[slot], g_recv.at[b], to)
 
-    def to_core(b, p, slot):
-        return remote(part(b, p), core_send.at[b, slot], core_recv.at[b, slot], (s, core_peer))
-
-    def to_chip(b, p):
-        return remote(part(b, p), chip_send.at[b], chip_recv.at[b], (s, chip_peer))
-
-    for k in range(1, sections):
-        direct(s, k - 1, ((s + k) % sections, d)).start()
+    def to_core(b, j):
+        return remote(
+            piece_of(b, q, q_chip, j), core_send.at[b, j], core_recv.at[b, j], (s, core_peer)
+        )
+
+    def from_core(b, j):
+        return remote(
+            piece_of(b, q_core, q_far, j), core_send.at[b, j], core_recv.at[b, j], (s, core_peer)
+        )
+
+    def to_chip(b, j):
+        return remote(piece_of(b, q, q_chip, j), chip_send.at[b, j], chip_recv.at[b, j], (s, chip_peer))
+
+    def from_chip(b, j):
+        return remote(
+            piece_of(b, q_chip, q_chip, j), chip_send.at[b, j], chip_recv.at[b, j], (s, chip_peer)
+        )
+
+    x_paced, y_paced = along_y < s, along_x < s
+    first = 2
+    for j in x_order[:first]:
+        own_x(j).start()
+    for j in y_order[:first]:
+        own_y(j).start()
+
+    @pl.when(jnp.logical_not(x_paced))
+    def _():
+        for j in x_order[first:]:
+            own_x(j).start()
+
+    @pl.when(jnp.logical_not(y_paced))
+    def _():
+        for j in y_order[first:]:
+            own_y(j).start()
+
     for k in range(1, sections):
         gain_copy(s, k - 1, ((s + k) % sections, d)).start()
 
-    def step1(b):
-        @pl.when(s != b)
-        def _():
-            direct(b, 0, (s, d)).wait_recv()
-            to_chip(b, q).start()
-            to_core(b, q, 0).start()
-
-    def step2(b):
-        @pl.when(s != b)
-        def _():
-            to_chip(b, q_chip).wait_recv()
-            to_core(b, q_chip, 1).start()
-
-    def step3(b):
+    def take(b, j):
+        atom(b, j, a_send.at[0, 0], (s, d)).wait_recv()
+
+    def spread(b, j):
+        if j < shared:
+            to_chip(b, j).start()
+        to_core(b, j).start()
+
+    def paced(i, order):
+        return order[first + i : first + i + 1] if i < len(even) - 1 else order[first + i :]
+
+    def gather():
+        for i in range(len(even)):
+            take(along_x, even[i])
+            relay_y(i).start()
+
+            @pl.when(y_paced)
+            def _():
+                for j in paced(i, y_order):
+                    own_y(j).start()
+
+            spread(along_x, even[i])
+            take(along_y, odd[i])
+            relay_x(i).start()
+
+            @pl.when(x_paced)
+            def _():
+                for j in paced(i, x_order):
+                    own_x(j).start()
+
+            spread(along_y, odd[i])
+        for i in range(len(even)):
+            take(along_x, odd[i])
+            spread(along_x, odd[i])
+            take(along_y, even[i])
+            spread(along_y, even[i])
+
+    def take_diagonal():
+        for j in range(atoms):
+            take(diagonal, j)
+            spread(diagonal, j)
+
+    def pass_on(b):
+        for j in range(shared):
+            from_chip(b, j).wait_recv()
+            to_core(b, atoms + j).start()
+
+    def at_hand(b):
         @pl.when(s != b)
         def _():
             gain_copy(b, 0, (s, d)).wait_recv()
-            to_core(b, q_core, 0).wait_recv()
-            to_core(b, q_far, 1).wait_recv()
+            for j in range(2 * mats):
+                from_core(b, j).wait_recv()
+
+    def late(cond):
+        @pl.when(cond)
+        def _():
+            take_diagonal()
+            pass_on(diagonal)
 
     pool_copy.wait()
     for i in range(per_section):
         for c in range(clips):
-            clip = idx_ref[s * per_section + i, c]
+            clip = idx_ref[c, s * per_section + i]
             for f in range(frames):
                 start = f * group + (i * clips + c) * SPATIAL
                 piece = pool[clip, f * SPATIAL : (f + 1) * SPATIAL, :]
@@ -169,7 +266,10 @@
     sums = [None] * per_section
 
     def quantize(v):
-        logits = jnp.dot(v, qw_ref[...], preferred_element_type=jnp.float32) + qb_ref[...]
+        logits = lax.dot_general(
+            v, qw_ref[...], (((1,), (1,)), ((), ())), preferred_element_type=jnp.float32
+        )
+        logits = logits + qb_ref[...]
         x = 4.0 * logits
         size = jnp.abs(x)
         e = jnp.exp(-size)
@@ -234,20 +334,18 @@
         loss_ref[...] = jnp.sum(jnp.where(wide == tall, loss, 0.0), axis=0, keepdims=True)
 
     hooks = {
-        (0, 0): lambda: step2(1),
-        (0, 1): lambda: step1(2),
-        (0, 2): lambda: step1(3),
-        (0, 3): lambda: (step2(2), step3(1)),
-        (1, 0): lambda: step2(3),
-        (1, 3): lambda: step3(2),
+        (0, 3): lambda: (late(diagonal == 1), at_hand(1)),
+        (1, 1): lambda: late(diagonal > 1),
+        (1, 3): lambda: at_hand(2),
         (2, 0): send_dp,
         (2, 2): send_all,
-        (2, 3): lambda: (start_all(), step3(3)),
+        (2, 3): lambda: (start_all(), at_hand(3)),
     }
-    step1(0)
-    step1(1)
-    step2(0)
-    step3(0)
+    gather()
+    late(diagonal == 0)
+    pass_on(along_x)
+    pass_on(along_y)
+    at_hand(0)
     errors = []
     for b in range(sections):
         src = source if b == 0 else current
@@ -284,18 +382,21 @@
 
     for k in range(1, sections):
         to = ((s + k) % sections, d)
-        direct(s, k - 1, to).wait_send()
         gain_copy(s, k - 1, to).wait_send()
         all_copy((s, k - 1), to).wait_send()
     for k in range(1, dps):
         dp_copy((d, k - 1), (s, (d + k) % dps)).wait_send()
-    for b in range(sections):
-
-        @pl.when(s != b)
-        def _():
-            to_chip(b, q).wait_send()
-            to_core(b, q, 0).wait_send()
-            to_core(b, q_chip, 1).wait_send()
+    for j in range(atoms):
+        own_x(j).wait_send()
+        own_y(j).wait_send()
+    for i in range(len(even)):
+        relay_x(i).wait_send()
+        relay_y(i).wait_send()
+    for b in (along_x, along_y, diagonal):
+        for j in range(2 * mats):
+            to_core(b, j).wait_send()
+        for j in range(shared):
+            to_chip(b, j).wait_send()
 
 
 def solution(mesh):
@@ -330,14 +431,15 @@
                 pltpu.VMEM((sections, per_section, 128), jnp.float32),
                 dma,
                 dma((mats,)),
+                dma((2, mats + mats // 2)),
+                dma((sections, mats + mats // 2)),
+                dma((2, mats)),
                 dma((sections - 1,)),
                 dma((sections,)),
-                dma((sections - 1,)),
-                dma((sections,)),
-                dma((sections, 2)),
-                dma((sections, 2)),
-                dma((sections,)),
-                dma((sections,)),
+                dma((sections, 2 * mats)),
+                dma((sections, 2 * mats)),
+                dma((sections, mats)),
+                dma((sections, mats)),
                 dma((dps - 1,)),
                 dma((dps,)),
                 dma((sections - 1,)),
@@ -346,7 +448,7 @@
             compiler_params=pltpu.CompilerParams(
                 collective_id=0, has_side_effects=True, vmem_limit_bytes=60 * 1024 * 1024
             ),
-        )(index, order, pool, taps, out_w, gain, qw, qb.reshape(1, -1), pw)
+        )(index.T, order, pool, taps, out_w, gain, qw.T, qb.reshape(1, -1), pw)
         return err, loss.reshape(batches)
 
     return jax.shard_map(

time: 92.7 us -> 71.6 us (0.77)
  Pallas kernels: 86.5 us -> 67.4 us
  local copies, waits for them, and re-layouts: 5.32 us -> 2.43 us
    pallas_call x1, Pallas kernels: 86.5 us -> 67.4 us  [on_device(): pl.pallas_call(functools.partial(kernel, sections, dps), out_shape=(jax.S...]
    unnamed x4 -> x2, local copies, waits for them, and re-layouts: 5.32 us -> 2.43 us
where the time goes in v2:
time: 71.6 us; the launch traced here: 70.5 us
  Pallas kernels  67.4 us (94%)
  local copies, waits for them, and re-layouts  2.43 us (3%)
    pallas_call x1, Pallas kernels, on_device(): pl.pallas_call(functools.partial(kernel, sections, dps), out_shape=(jax.S...  67.4 us
    unnamed x2, local copies, waits for them, and re-layouts  2.43 us

profile of v2, /device:TPU:0, one launch (start us, length us, event | category | flops | bytes accessed | tf_op | source)
XLA Modules:
  0.0 70.5 jit_solution(15344627639491127578)
XLA Ops:
  0.6 67.4 %shard_map.104 = (f32[2,4,256]{2,1,0:T(4,128)}, f32[1,8]{1,0:T(1,128)}) custom-call(s32[4,8]{1,0:T(4,128)} %bitcast.5, s32[8]{0:T(128)} %order_ref.1, bf16[32,256,512]{2,1,0:T(8,128)(2,1)} %pool_ref.1, bf16[1,3,512,512]{3,2,1,0:T(8,128)(2,1)} %taps_ref.1, bf16[1,512,512]{2,1,0:T(8,128)(2,1)} %out_w_ref.1, bf16[1,512]{1,0:T(2,128)(2,1)} %gain_ref.1, ...), custom_call_target="tpu_custom_call" | custom-call | tf_op jit(solution)/shard_map/pallas_call | solution.py:415
  68.1 1.3 %copy.13 = f32[2,4,256]{2,1,0:T(4,128)} copy(f32[2,4,256]{2,1,0:T(4,128)} %get-tuple-element.8) | data formatting | bytes 16384
  69.4 1.1 %copy.14 = f32[8]{0:T(128)} copy(f32[8]{0:T(128)} %bitcast.7) | data formatting | bytes 64

commit v3 on v2

--- a/solution.py
+++ b/solution.py
@@ -208,21 +208,22 @@
                     own_x(j).start()
 
             spread(along_y, odd[i])
-        for i in range(len(even)):
-            take(along_x, odd[i])
-            spread(along_x, odd[i])
-            take(along_y, even[i])
-            spread(along_y, even[i])
-
-    def take_diagonal():
-        for j in range(atoms):
-            take(diagonal, j)
-            spread(diagonal, j)
+
+    def rest(b):
+        for source_block, order in ((along_x, odd), (along_y, even), (diagonal, even + odd)):
+
+            @pl.when(source_block == b)
+            def _():
+                for j in order:
+                    take(b, j)
+                    spread(b, j)
 
     def pass_on(b):
-        for j in range(shared):
-            from_chip(b, j).wait_recv()
-            to_core(b, atoms + j).start()
+        @pl.when(s != b)
+        def _():
+            for j in range(shared):
+                from_chip(b, j).wait_recv()
+                to_core(b, atoms + j).start()
 
     def at_hand(b):
         @pl.when(s != b)
@@ -230,12 +231,6 @@
             gain_copy(b, 0, (s, d)).wait_recv()
             for j in range(2 * mats):
                 from_core(b, j).wait_recv()
-
-    def late(cond):
-        @pl.when(cond)
-        def _():
-            take_diagonal()
-            pass_on(diagonal)
 
     pool_copy.wait()
     for i in range(per_section):
@@ -334,17 +329,20 @@
         loss_ref[...] = jnp.sum(jnp.where(wide == tall, loss, 0.0), axis=0, keepdims=True)
 
     hooks = {
-        (0, 3): lambda: (late(diagonal == 1), at_hand(1)),
-        (1, 1): lambda: late(diagonal > 1),
+        (0, 0): lambda: rest(1),
+        (0, 1): lambda: pass_on(1),
+        (0, 3): lambda: at_hand(1),
+        (1, 0): lambda: rest(2),
+        (1, 1): lambda: pass_on(2),
         (1, 3): lambda: at_hand(2),
-        (2, 0): send_dp,
+        (2, 0): lambda: (send_dp(), rest(3)),
+        (2, 1): lambda: pass_on(3),
         (2, 2): send_all,
         (2, 3): lambda: (start_all(), at_hand(3)),
     }
     gather()
-    late(diagonal == 0)
-    pass_on(along_x)
-    pass_on(along_y)
+    rest(0)
+    pass_on(0)
     at_hand(0)
     errors = []
     for b in range(sections):

time: 71.6 us -> 68.3 us (0.954); the launches traced: 70.5 us -> 68 us
  Pallas kernels: 67.4 us -> 65 us
    pallas_call x1, Pallas kernels: 67.4 us -> 65 us  [on_device(): pl.pallas_call(functools.partial(kernel, sections, dps), out_shape=(jax.S...]
where the time goes in v3:
time: 68.3 us; the launch traced here: 68 us
  Pallas kernels  65 us (95%)
  local copies, waits for them, and re-layouts  2.43 us (4%)
    pallas_call x1, Pallas kernels, on_device(): pl.pallas_call(functools.partial(kernel, sections, dps), out_shape=(jax.S...  65 us
    unnamed x2, local copies, waits for them, and re-layouts  2.43 us

profile of v3, /device:TPU:0, one launch (start us, length us, event | category | flops | bytes accessed | tf_op | source)
XLA Modules:
  0.0 68.0 jit_solution(11335851573781243142)
XLA Ops:
  0.6 65.0 %shard_map.104 = (f32[2,4,256]{2,1,0:T(4,128)}, f32[1,8]{1,0:T(1,128)}) custom-call(s32[4,8]{1,0:T(4,128)} %bitcast.5, s32[8]{0:T(128)} %order_ref.1, bf16[32,256,512]{2,1,0:T(8,128)(2,1)} %pool_ref.1, bf16[1,3,512,512]{3,2,1,0:T(8,128)(2,1)} %taps_ref.1, bf16[1,512,512]{2,1,0:T(8,128)(2,1)} %out_w_ref.1, bf16[1,512]{1,0:T(2,128)(2,1)} %gain_ref.1, ...), custom_call_target="tpu_custom_call" | custom-call | tf_op jit(solution)/shard_map/pallas_call | solution.py:413
  65.6 1.3 %copy.13 = f32[2,4,256]{2,1,0:T(4,128)} copy(f32[2,4,256]{2,1,0:T(4,128)} %get-tuple-element.8) | data formatting | bytes 16384
  66.9 1.1 %copy.14 = f32[8]{0:T(128)} copy(f32[8]{0:T(128)} %bitcast.7) | data formatting | bytes 64
